TPU v7x, 32 devices: a whole 2x2x4 slice. The times are simulated.
32 devices in a mesh: gx: 4 (over y, core), gy: 8 (over z, x).
Axes of the slice: x: 2, y: 2, z: 4, core: 2. Of those that a mesh axis runs over, the one named last changes fastest.
Arguments:
- wavefield: float32 [8, 16, 3, 125, 256], P('gx', 'gy'), may hold values from -0.6 to 0.6
- moduli: float32 [8, 16, 2, 256], P('gx', 'gy'), may hold values from 0.5 to 4
- residuals: float32 [32, 32, 128], P(('gx', 'gy')), may hold values from -6 to 6
- coords: float32 [32, 32, 3, 128], P(('gx', 'gy')), may hold values from -1 to 1
- angles: float32 [32, 32, 2, 128], P(('gx', 'gy')), may hold values from -3.140625 to 3.140625
- element_ids: int32 [32, 32, 128], P(('gx', 'gy')), may hold values from 0 to 1023
- counts: int32 [32, 32], P(('gx', 'gy')), may hold values from 0 to 128, as said below
Outputs:
- force: float32 [8, 16, 3, 125, 256], P('gx', 'gy')
Inputs may be any that keep to these rules, and one draw needn't show every extreme that they name: `counts`: each sending device has at least one tile with exactly 128 live slots; in every draw one owner receives 128 live slots from every sender. The lightest owners receive on average about a sixth of 128 a sender, the others lie between.
All inputs are finite; a program needn't handle non-finite values.
Results may differ from a plain program's by a relative error of at most 0.0003.
Values sent between devices are 32-bit elements; how exact they have to be, the bound alone decides.
A program may use at most 64 MiB of HBM per device.

v0:
```python
import math
import jax
import jax.numpy as jnp
import numpy as np
from jax import lax
from jax.sharding import PartitionSpec as P


def with_halo(block, sides, width):
    for axis, dim in sides:
        count = lax.axis_size(axis)
        forward = [(i, i + 1) for i in range(count - 1)]
        backward = [(target, source) for source, target in forward]
        low = lax.ppermute(
            lax.slice_in_dim(block, block.shape[dim] - width, None, axis=dim), axis, forward
        )
        high = lax.ppermute(lax.slice_in_dim(block, 0, width, axis=dim), axis, backward)
        block = jnp.concatenate([low, block, high], axis=dim)
    return block


def gll_points():
    return np.array([-1.0, -math.sqrt(3.0 / 7.0), 0.0, math.sqrt(3.0 / 7.0), 1.0])


def gll_weights():
    return np.array([0.1, 49.0 / 90.0, 32.0 / 45.0, 49.0 / 90.0, 0.1])


def derivative_table():
    points = gll_points()
    table = np.zeros((5, 5))
    for row in range(5):
        for col in range(5):
            if row == col:
                table[row, col] = sum(
                    (1.0 / (points[col] - points[other]) for other in range(5) if other != col)
                )
            else:
                value = 1.0 / (points[col] - points[row])
                for other in range(5):
                    if other != col and other != row:
                        value = (
                            value * (points[row] - points[other]) / (points[col] - points[other])
                        )
                table[row, col] = value
    return table


def basis(where):
    points = gll_points()
    values = []
    slopes = []
    for node in range(5):
        value = jnp.ones_like(where)
        slope = jnp.zeros_like(where)
        for other in range(5):
            if other != node:
                scale = 1.0 / (points[node] - points[other])
                factor = (where - points[other]) * scale
                slope = slope * factor + value * scale
                value = value * factor
        values.append(value)
        slopes.append(slope)
    return (jnp.stack(values), jnp.stack(slopes))


def sources(resid, coord, angle, live_count):
    slots = resid.shape[-1]
    live = jnp.arange(slots, dtype=jnp.int32)[None, :] < live_count[:, None]
    value = jnp.where(live, resid, 0.0).reshape(-1)
    first = coord[:, 0, :].reshape(-1)
    second = coord[:, 1, :].reshape(-1)
    third = coord[:, 2, :].reshape(-1)
    azimuth = angle[:, 0, :].reshape(-1)
    dip = angle[:, 1, :].reshape(-1)
    tang_x = jnp.cos(azimuth) * jnp.cos(dip)
    tang_y = jnp.sin(azimuth) * jnp.cos(dip)
    tang_z = jnp.sin(dip)
    val_x, der_x = basis(first)
    val_y, der_y = basis(second)
    val_z, der_z = basis(third)
    shape = (
        tang_x * der_x[:, None, None, :] * val_y[None, :, None, :] * val_z[None, None, :, :]
        + tang_y * val_x[:, None, None, :] * der_y[None, :, None, :] * val_z[None, None, :, :]
        + tang_z * val_x[:, None, None, :] * val_y[None, :, None, :] * der_z[None, None, :, :]
    )
    direction = jnp.stack([tang_x, tang_y, tang_z]) * value[None, :]
    return (direction[:, None, None, None, :] * shape[None]).reshape(375, -1)


def along(field, table, dim):
    if dim == 0:
        return jnp.einsum("pa,...aqsz->...pqsz", table, field, precision=lax.Precision.HIGHEST)
    if dim == 1:
        return jnp.einsum("qb,...pbsz->...pqsz", table, field, precision=lax.Precision.HIGHEST)
    return jnp.einsum("sc,...pqcz->...pqsz", table, field, precision=lax.Precision.HIGHEST)


def back(field, table, dim):
    if dim == 0:
        return jnp.einsum("pa,...pqsz->...aqsz", table, field, precision=lax.Precision.HIGHEST)
    if dim == 1:
        return jnp.einsum("qb,...pqsz->...pbsz", table, field, precision=lax.Precision.HIGHEST)
    return jnp.einsum("sc,...pqsz->...pqcz", table, field, precision=lax.Precision.HIGHEST)


def stiffness(field, moduli):
    table = jnp.asarray(derivative_table(), jnp.float32)
    weight = jnp.asarray(gll_weights(), jnp.float32)
    wgrid = (weight[:, None, None] * weight[None, :, None] * weight[None, None, :])[:, :, :, None]
    grads = [along(field, table, dim) for dim in range(3)]
    lame = moduli[..., 0, :][..., None, None, None, :]
    shear = moduli[..., 1, :][..., None, None, None, :]
    diverge = (
        grads[0][..., 0, :, :, :, :] + grads[1][..., 1, :, :, :, :] + grads[2][..., 2, :, :, :, :]
    )
    result = jnp.zeros_like(field)
    for col in range(3):
        parts = []
        for row in range(3):
            stress = shear * (grads[col][..., row, :, :, :, :] + grads[row][..., col, :, :, :, :])
            if row == col:
                stress = stress + lame * diverge
            parts.append(stress * wgrid)
        result = result + back(jnp.stack(parts, axis=-5), table, col)
    return result


def assemble_dim(field, e_dim, n_dim, fetch):
    count = field.shape[e_dim]
    low = lax.slice_in_dim(field, 0, 1, axis=n_dim)
    high = lax.slice_in_dim(field, 4, 5, axis=n_dim)
    middle = lax.slice_in_dim(field, 1, 4, axis=n_dim)
    first = lax.slice_in_dim(low, 0, 1, axis=e_dim)
    last = lax.slice_in_dim(high, count - 1, count, axis=e_dim)
    below, above = fetch(first, last)
    low_next = jnp.concatenate([lax.slice_in_dim(low, 1, count, axis=e_dim), above], axis=e_dim)
    high_prev = jnp.concatenate(
        [below, lax.slice_in_dim(high, 0, count - 1, axis=e_dim)], axis=e_dim
    )
    return jnp.concatenate([low + high_prev, middle, high + low_next], axis=n_dim)


def fetch_none(first, last):
    return (jnp.zeros_like(last), jnp.zeros_like(first))


def fetch_first(first, last):
    padded = with_halo(jnp.concatenate([first, last], axis=0), (("gx", 0),), 1)
    return (padded[0:1], padded[3:4])


def fetch_second(first, last):
    padded = with_halo(jnp.concatenate([first, last], axis=1), (("gy", 1),), 1)
    return (padded[:, 0:1], padded[:, 3:4])


def body(wavefield, moduli, residuals, coords, angles, element_ids, counts):
    cells_x = wavefield.shape[0]
    cells_y = wavefield.shape[1]
    depth = wavefield.shape[4]
    groups_x = lax.axis_size("gx")
    groups_y = lax.axis_size("gy")
    owners = groups_x * groups_y
    slots = residuals.shape[2]
    blocks = owners // 16
    elements = cells_x * cells_y * depth
    field = wavefield.reshape(cells_x, cells_y, 3, 5, 5, 5, depth)
    internal = stiffness(field, moduli)
    floats = (
        lax.all_to_all(residuals, ("gx", "gy"), split_axis=1, concat_axis=0, tiled=True),
        lax.all_to_all(coords, ("gx", "gy"), split_axis=1, concat_axis=0, tiled=True),
        lax.all_to_all(angles, ("gx", "gy"), split_axis=1, concat_axis=0, tiled=True),
    )
    index = (
        lax.all_to_all(element_ids, ("gx", "gy"), split_axis=1, concat_axis=0, tiled=True),
        lax.all_to_all(counts, ("gx", "gy"), split_axis=1, concat_axis=0, tiled=True),
    )
    got_resid = floats[0].reshape(blocks, 16, slots)
    got_coord = floats[1].reshape(blocks, 16, 3, slots)
    got_angle = floats[2].reshape(blocks, 16, 2, slots)
    got_ids = index[0].reshape(blocks, 16, slots)
    got_count = index[1].reshape(blocks, 16)
    numbers = jnp.arange(elements, dtype=jnp.int32)

    def add_block(step, total):
        contrib = sources(got_resid[step], got_coord[step], got_angle[step], got_count[step])
        onehot = (got_ids[step].reshape(-1)[:, None] == numbers[None, :]).astype(jnp.float32)
        onehot = onehot.reshape(-1, cells_x, cells_y, depth)
        return total + jnp.einsum("ks,sxyz->xykz", contrib, onehot, precision=lax.Precision.HIGHEST)

    start = jnp.zeros((cells_x, cells_y, 375, depth), jnp.float32)
    total = lax.fori_loop(0, blocks, add_block, start)
    injected = total.reshape(cells_x, cells_y, 3, 5, 5, 5, depth)
    force = injected - internal
    force = assemble_dim(force, 0, 3, fetch_first)
    force = assemble_dim(force, 1, 4, fetch_second)
    force = assemble_dim(force, 6, 5, fetch_none)
    return force.reshape(cells_x, cells_y, 3, 125, depth)


def solution(mesh):
    in_specs = (
        P("gx", "gy", None, None, None),
        P("gx", "gy", None, None),
        P(("gx", "gy"), None, None),
        P(("gx", "gy"), None, None, None),
        P(("gx", "gy"), None, None, None),
        P(("gx", "gy"), None, None),
        P(("gx", "gy"), None),
    )
    out_specs = P("gx", "gy", None, None, None)
    return jax.shard_map(body, mesh=mesh, in_specs=in_specs, out_specs=out_specs, check_vma=False)
```

profile of v0, /device:TPU:9, one launch (start us, length us, event | category | flops | bytes accessed | tf_op | source)
XLA Modules:
  0.0 154.2 jit_solution(17965460843285024868)
XLA Ops:
  1.5 6.3 %all-to-all-start.2 = ((s32[1,32,1]{2,0,1:T(1,128)}), s32[1,32,1]{2,0,1:T(1,128)S(1)}, u32[]{:S(2)}, u32[]{:S(2)}) async-start(s32[1,32,1]{2,0,1:T(1,128)} %copy.67), calls=%async_computation.2 | async-start | bytes 32768 | tf_op jit(solution)/shard_map/all_to_all | solution.py:178
  7.8 3.1 %fusion.33 = f32[5,2,2,3,5,5,256]{6,0,5,4,3,2,1:T(8,128)S(1)} fusion(f32[5,5,1,1,1,1,1]{1,0,6,5,4,3,2:T(8,128)} %constant.255, f32[2,2,3,5,5,5,256]{6,1,5,4,3,2,0:T(2,128)S(1)} %bitcast.111), kind=kOutput, calls=%fused_computation.120 | convolution fusion | flops 23040000 | bytes 3072100 | tf_op jit(solution)/shard_map/sc,...pqcz->...pqsz/dot_general | solution.py:97
  20.2 5.9 %all-to-all-start.3 = ((f32[1,32,128]{2,0,1:T(1,128)}), f32[1,32,128]{2,0,1:T(1,128)}, u32[]{:S(2)}, u32[]{:S(2)}) async-start(f32[1,32,128]{2,0,1:T(1,128)} %bitcast.5), calls=%async_computation.3 | async-start | bytes 32768 | tf_op jit(solution)/shard_map/all_to_all | solution.py:172
  26.1 3.1 %add_multiply_fusion.1 = (f32[2,2,1,5,5,5,256]{6,3,5,4,2,1,0:T(8,128)}, f32[2,2,1,5,5,5,256]{6,3,5,4,2,1,0:T(8,128)}) fusion(f32[2,2,1,5,5,5,256]{6,3,5,4,2,1,0:T(8,128)} %get-tuple-element.358, f32[2,2,3,5,5,5,256]{6,3,5,4,2,1,0:T(8,128)} %bitcast.115, f32[5,5,5]{0,2,1:T(8,128)S(1)} %broadcast_multiply_fusion.8, f32[2,2,256]{2,1,0:T(2,128)S(1)} %get-tuple-element.425, ...), kind=kLoop, calls=%fused_computation.138 | loop fusion | flops 1024000 | bytes 2564596 | tf_op jit(solution)/shard_map/mul | solution.py:125
  29.1 2.5 %all-to-all-done.3 = f32[1,32,128]{2,0,1:T(1,128)} async-done(((f32[1,32,128]{2,0,1:T(1,128)}), f32[1,32,128]{2,0,1:T(1,128)}, u32[]{:S(2)}, u32[]{:S(2)}) %all-to-all-start.3) | async-done | bytes 16416 | tf_op jit(solution)/shard_map/all_to_all | solution.py:172
  31.7 4.5 %all-to-all-start = ((s32[1,32,128]{2,0,1:T(1,128)}), s32[1,32,128]{2,0,1:T(1,128)}, u32[]{:S(2)}, u32[]{:S(2)}) async-start(s32[1,32,128]{2,0,1:T(1,128)} %bitcast), calls=%async_computation | async-start | bytes 32768 | tf_op jit(solution)/shard_map/all_to_all | solution.py:177
  36.2 4.6 %pad_maximum_fusion = (f32[2,2,3,5,5,5,256]{6,3,5,4,2,1,0:T(8,128)}, f32[2,2,3,5,5,5,256]{6,3,5,4,2,1,0:T(8,128)}) fusion(f32[2,2,1,5,5,5,256]{6,3,5,4,2,1,0:T(8,128)} %get-tuple-element.403, f32[2,2,1,5,5,5,256]{6,3,5,4,2,1,0:T(8,128)} %get-tuple-element.418, f32[2,2,1,5,5,5,256]{6,3,5,4,2,1,0:T(8,128)S(1)} %get-tuple-element.401, ...), kind=kLoop, calls=%fused_computation.107 | loop fusion | flops 1536000 | bytes 5632000 | tf_op jit(solution)/shard_map/stack | solution.py:126
  41.8 5.6 %all-to-all-start.4 = ((f32[1,32,3,128]{3,2,0,1:T(4,128)}), f32[1,32,3,128]{3,2,0,1:T(4,128)S(1)}, u32[]{:S(2)}, u32[]{:S(2)}) async-start(f32[1,32,3,128]{3,2,0,1:T(4,128)} %copy.69), calls=%async_computation.4 | async-start | bytes 131072 | tf_op jit(solution)/shard_map/all_to_all | solution.py:173
  47.4 5.9 %fusion.31 = f32[2,2,3,5,5,256,5]{5,6,4,3,2,1,0:T(8,128)} fusion(f32[5,5,1,1,1,1,1]{1,0,6,5,4,3,2:T(8,128)S(1)} %copy-done.9, f32[2,2,3,5,5,5,256]{6,3,5,4,2,1,0:T(8,128)} %get-tuple-element.420), kind=kOutput, calls=%fused_computation.117 | convolution fusion | flops 23040000 | bytes 3072100 | tf_op jit(solution)/shard_map/qb,...pqsz->...pbsz/dot_general | solution.py:104
  53.3 5.8 %all-to-all-start.1 = ((f32[1,32,2,128]{3,2,0,1:T(2,128)}), f32[1,32,2,128]{3,2,0,1:T(2,128)S(1)}, u32[]{:S(2)}, u32[]{:S(2)}) async-start(f32[1,32,2,128]{3,2,0,1:T(2,128)} %bitcast.2), calls=%async_computation.1 | async-start | bytes 65536 | tf_op jit(solution)/shard_map/all_to_all | solution.py:174
  59.1 5.9 %fusion.29 = f32[2,2,3,5,5,256,5]{5,6,4,3,2,1,0:T(8,128)} fusion(f32[5,5,1,1,1,1,1]{1,0,6,5,4,3,2:T(8,128)S(1)} %copy-done.9, f32[2,2,3,5,5,5,256]{6,3,5,4,2,1,0:T(8,128)} %get-tuple-element.421), kind=kOutput, calls=%fused_computation.115 | convolution fusion | flops 23040000 | bytes 3072100 | tf_op jit(solution)/shard_map/sc,...pqsz->...pqcz/dot_general | solution.py:105
  65.8 52.7 %while.17 = (s32[]{:T(128)}, f32[2,2,375,256]{3,2,1,0:T(8,128)}, s32[2,16,128]{2,1,0:T(8,128)}, f32[2,16,2,128]{3,2,1,0:T(2,128)S(1)}, s32[2,16]{1,0:T(2,128)S(1...) while((s32[]{:T(128)}, f32[2,2,375,256]{3,2,1,0:T(8,128)}, ...), condition=%wide.region_1.2_spmd.clone, body=%wide.region_0.1_spmd.clone.sunk | while | flops 9442392064 | bytes 20555300 | solution.py:194
  75.5 2.9 %broadcast_multiply_fusion.15 = f32[3,5,5,5,2048]{4,3,2,1,0:T(8,128)} fusion(f32[5,5,5,2048]{3,2,1,0:T(8,128)S(1)} %multiply_add_fusion.22, f32[3,2048]{1,0:T(4,128)S(1)} %maximum_multiply_fusion.2), kind=kLoop, calls=%fused_computation.6.clone.1 | loop fusion | flops 768000 | bytes 4120576 | tf_op jit(solution)/shard_map/while/body/eval_jaxpr/mul | solution.py:89
  78.4 5.1 %reshape.2477 = f32[375,2048,1,1]{1,0,2,3:T(8,128)} reshape(f32[3,5,5,5,2048]{4,3,2,1,0:T(8,128)} %broadcast_multiply_fusion.15) | data formatting | bytes 6144000 | tf_op jit(solution)/shard_map/while/body/eval_jaxpr/mul | solution.py:89
  83.4 8.3 %bitcast_add_fusion.4 = f32[2,2,375,256]{3,2,1,0:T(8,128)} fusion(f32[2,2,375,256]{3,2,1,0:T(8,128)} %get-tuple-element.563, f32[375,2048,1,1]{1,0,2,3:T(8,128)} %reshape.2477, s32[2,2,256]{2,1,0:T(2,128)S(1)} %copy-done.10, s32[2048]{0:T(1024)S(1)} %copy-done.8, pred[]{:T(512)S(6)} %compare.5), kind=kOutput, calls=%fused_computation.8.clone.1 | convolution fusion | flops 9440049152 | bytes 6156289 | tf_op jit(solution)/shard_map/while/body/eval_jaxpr/ks,sxyz->xykz/dot_general | solution.py:191
  101.5 2.9 %broadcast_multiply_fusion.15 = f32[3,5,5,5,2048]{4,3,2,1,0:T(8,128)} fusion(f32[5,5,5,2048]{3,2,1,0:T(8,128)S(1)} %multiply_add_fusion.22, f32[3,2048]{1,0:T(4,128)S(1)} %maximum_multiply_fusion.2), kind=kLoop, calls=%fused_computation.6.clone.1 | loop fusion | flops 768000 | bytes 4120576 | tf_op jit(solution)/shard_map/while/body/eval_jaxpr/mul | solution.py:89
  104.4 5.1 %reshape.2477 = f32[375,2048,1,1]{1,0,2,3:T(8,128)} reshape(f32[3,5,5,5,2048]{4,3,2,1,0:T(8,128)} %broadcast_multiply_fusion.15) | data formatting | bytes 6144000 | tf_op jit(solution)/shard_map/while/body/eval_jaxpr/mul | solution.py:89
  109.5 8.8 %bitcast_add_fusion.4 = f32[2,2,375,256]{3,2,1,0:T(8,128)} fusion(f32[2,2,375,256]{3,2,1,0:T(8,128)} %get-tuple-element.563, f32[375,2048,1,1]{1,0,2,3:T(8,128)} %reshape.2477, s32[2,2,256]{2,1,0:T(2,128)S(1)} %copy-done.10, s32[2048]{0:T(1024)S(1)} %copy-done.8, pred[]{:T(512)S(6)} %compare.5), kind=kOutput, calls=%fused_computation.8.clone.1 | convolution fusion | flops 9440049152 | bytes 6156289 | tf_op jit(solution)/shard_map/while/body/eval_jaxpr/ks,sxyz->xykz/dot_general | solution.py:191
  120.9 5.7 %fusion.28 = f32[2,2,3,5,5,5,256]{6,3,5,4,2,1,0:T(8,128)S(1)} fusion(f32[2,2,3,5,5,5,256]{6,1,5,4,3,2,0:T(2,128)S(1)} %bitcast.116, f32[2,2,3,5,5,256,5]{5,6,4,3,2,1,0:T(8,128)} %fusion.29, f32[2,2,3,5,5,256,5]{5,6,4,3,2,1,0:T(8,128)S(1)} %copy-done.3, f32[5,5,1,1,1,1,1]{1,0,6,5,4,3,2:T(8,128)S(1)} %copy-done.9, ...), kind=kOutput, calls=%fused_computation.113 | convolution fusion | flops 24960000 | bytes 7680100 | tf_op jit(solution)/shard_map/pa,...pqsz->...aqsz/dot_general | solution.py:102
  127.1 3.4 %collective-permute-start = (f32[1,2,3,1,5,5,256]{6,3,5,4,2,1,0:T(1,128)S(1)}, f32[1,2,3,1,5,5,256]{6,3,5,4,2,1,0:T(1,128)S(1)}, u32[]{:S(2)}, u32[]{:S(2)}) collective-permute-start(f32[1,2,3,1,5,5,256]{6,3,5,4,2,1,0:T(1,128)S(1)} %get-tuple-element.412), channel_id=1, source_target_pairs={{0,8},{8,16},{16,24},{1,9},{9,17},{17,25},{2,10},{10,18},{18,26},{... | collective-permute-start | bytes 460808 | tf_op jit(solution)/shard_map/ppermute | solution.py:14
  132.7 4.3 %collective-permute-done.1 = f32[1,2,3,1,5,5,256]{6,3,5,4,2,1,0:T(1,128)S(1)} collective-permute-done((f32[1,2,3,1,5,5,256]{6,3,5,4,2,1,0:T(1,128)S(1)}, f32[1,2,3,1,5,5,256]{6,3,5,4,2,1,0:T(1,128)S(1)}, u32[]{:S(2)}, u32[]{:S(2)}) %collective-permute-start.1) | collective-permute-done | bytes 153632 | tf_op jit(solution)/shard_map/ppermute | solution.py:17
  138.0 3.1 %collective-permute-start.2 = (f32[2,1,3,5,1,5,256]{6,3,5,4,2,1,0:T(8,128)S(1)}, f32[2,1,3,5,1,5,256]{6,3,5,4,2,1,0:T(8,128)S(1)}, u32[]{:S(2)}, u32[]{:S(2)}) collective-permute-start(f32[2,1,3,5,1,5,256]{6,3,5,4,2,1,0:T(8,128)S(1)} %get-tuple-element.416), channel_id=1, source_target_pairs={{0,1},{1,2},{2,3},{3,4},{4,5},{5,6},{6,7},{8,9},{9,10},{10,11},{11... | collective-permute-start | bytes 460808 | tf_op jit(solution)/shard_map/ppermute | solution.py:14
  141.1 3.1 %collective-permute-start.3 = (f32[2,1,3,5,1,5,256]{6,3,5,4,2,1,0:T(8,128)S(1)}, f32[2,1,3,5,1,5,256]{6,3,5,4,2,1,0:T(8,128)S(1)}, u32[]{:S(2)}, u32[]{:S(2)}) collective-permute-start(f32[2,1,3,5,1,5,256]{6,3,5,4,2,1,0:T(8,128)S(1)} %get-tuple-element.417), channel_id=1, source_target_pairs={{1,0},{2,1},{3,2},{4,3},{5,4},{6,5},{7,6},{9,8},{10,9},{11,10},{12... | collective-permute-start | bytes 460808 | tf_op jit(solution)/shard_map/ppermute | solution.py:17
  145.1 4.4 %collective-permute-done.2 = f32[2,1,3,5,1,5,256]{6,3,5,4,2,1,0:T(8,128)S(1)} collective-permute-done((f32[2,1,3,5,1,5,256]{6,3,5,4,2,1,0:T(8,128)S(1)}, f32[2,1,3,5,1,5,256]{6,3,5,4,2,1,0:T(8,128)S(1)}, u32[]{:S(2)}, u32[]{:S(2)}) %collective-permute-start.2) | collective-permute-done | bytes 153632 | tf_op jit(solution)/shard_map/ppermute | solution.py:14
  (128 shorter events, 43.4 us)
Async XLA Ops:
  0.0 7.8 %copy-start = (f32[2,2,3,125,256]{4,1,3,2,0:T(2,128)S(1)}, f32[2,2,3,125,256]{4,1,3,2,0:T(2,128)}, u32[]{:S(2)}) copy-start(f32[2,2,3,125,256]{4,1,3,2,0:T(2,128)} %param.11) | copy-start | bytes 4608004
  1.5 18.7 %all-to-all-start.2 = ((s32[1,32,1]{2,0,1:T(1,128)}), s32[1,32,1]{2,0,1:T(1,128)S(1)}, u32[]{:S(2)}, u32[]{:S(2)}) async-start(s32[1,32,1]{2,0,1:T(1,128)} %copy.67), calls=%async_computation.2 | async-start | bytes 32768 | tf_op jit(solution)/shard_map/all_to_all | solution.py:178
  20.2 11.5 %all-to-all-start.3 = ((f32[1,32,128]{2,0,1:T(1,128)}), f32[1,32,128]{2,0,1:T(1,128)}, u32[]{:S(2)}, u32[]{:S(2)}) async-start(f32[1,32,128]{2,0,1:T(1,128)} %bitcast.5), calls=%async_computation.3 | async-start | bytes 32768 | tf_op jit(solution)/shard_map/all_to_all | solution.py:172
  31.7 10.2 %all-to-all-start = ((s32[1,32,128]{2,0,1:T(1,128)}), s32[1,32,128]{2,0,1:T(1,128)}, u32[]{:S(2)}, u32[]{:S(2)}) async-start(s32[1,32,128]{2,0,1:T(1,128)} %bitcast), calls=%async_computation | async-start | bytes 32768 | tf_op jit(solution)/shard_map/all_to_all | solution.py:177
  36.2 4.6 %copy-start.11 = (f32[1,32,3,128]{3,1,2,0:T(8,128)S(1)}, f32[1,32,3,128]{3,1,2,0:T(8,128)}, u32[]{:S(2)}) copy-start(f32[1,32,3,128]{3,1,2,0:T(8,128)} %param.14) | copy-start | bytes 147460
  41.8 11.5 %all-to-all-start.4 = ((f32[1,32,3,128]{3,2,0,1:T(4,128)}), f32[1,32,3,128]{3,2,0,1:T(4,128)S(1)}, u32[]{:S(2)}, u32[]{:S(2)}) async-start(f32[1,32,3,128]{3,2,0,1:T(4,128)} %copy.69), calls=%async_computation.4 | async-start | bytes 131072 | tf_op jit(solution)/shard_map/all_to_all | solution.py:173
  53.3 12.5 %all-to-all-start.1 = ((f32[1,32,2,128]{3,2,0,1:T(2,128)}), f32[1,32,2,128]{3,2,0,1:T(2,128)S(1)}, u32[]{:S(2)}, u32[]{:S(2)}) async-start(f32[1,32,2,128]{3,2,0,1:T(2,128)} %bitcast.2), calls=%async_computation.1 | async-start | bytes 65536 | tf_op jit(solution)/shard_map/all_to_all | solution.py:174
  65.8 4.3 %copy-start.4 = (f32[2,16,3,128]{3,1,2,0:T(8,128)}, f32[2,16,3,128]{3,1,2,0:T(8,128)S(1)}, u32[]{:S(2)}) copy-start(f32[2,16,3,128]{3,1,2,0:T(8,128)S(1)} %get-tuple-element.577) | copy-start | bytes 147460 | tf_op jit(solution)/shard_map/while
  65.8 4.3 %copy-start.6 = (f32[2,16,2,128]{3,2,1,0:T(2,128)}, f32[2,16,2,128]{3,2,1,0:T(2,128)S(1)}, u32[]{:S(2)}) copy-start(f32[2,16,2,128]{3,2,1,0:T(2,128)S(1)} %get-tuple-element.574) | copy-start | bytes 98308 | tf_op jit(solution)/shard_map/while
  78.4 5.1 %copy-start.8 = (s32[2048]{0:T(1024)S(1)}, s32[2048]{0:T(1024)}, u32[]{:S(2)}) copy-start(s32[2048]{0:T(1024)} %dynamic-slice_bitcast_fusion.5) | copy-start | bytes 24580 | tf_op jit(solution)/shard_map/while
  78.4 5.1 %copy-start.10 = (s32[2,2,256]{2,1,0:T(2,128)S(1)}, s32[2,2,256]{2,1,0:T(2,128)}, u32[]{:S(2)}) copy-start(s32[2,2,256]{2,1,0:T(2,128)} %multiply_add_fusion.23) | copy-start | bytes 12292 | tf_op jit(solution)/shard_map/while
  83.4 8.4 %copy-start.5 = (f32[2,16,3,128]{3,1,2,0:T(8,128)S(1)}, f32[2,16,3,128]{3,1,2,0:T(8,128)}, u32[]{:S(2)}) copy-start(f32[2,16,3,128]{3,1,2,0:T(8,128)} %copy-done.4) | copy-start | bytes 147460 | tf_op jit(solution)/shard_map/while
  83.4 8.4 %copy-start.7 = (f32[2,16,2,128]{3,2,1,0:T(2,128)S(1)}, f32[2,16,2,128]{3,2,1,0:T(2,128)}, u32[]{:S(2)}) copy-start(f32[2,16,2,128]{3,2,1,0:T(2,128)} %copy-done.6) | copy-start | bytes 98308 | tf_op jit(solution)/shard_map/while
  83.4 8.4 %copy-start.15 = (s32[2,16]{1,0:T(2,128)S(1)}, s32[2,16]{1,0:T(2,128)}, u32[]{:S(2)}) copy-start(s32[2,16]{1,0:T(2,128)} %copy-done.14) | copy-start | bytes 388 | tf_op jit(solution)/shard_map/while
  91.8 4.3 %copy-start.4 = (f32[2,16,3,128]{3,1,2,0:T(8,128)}, f32[2,16,3,128]{3,1,2,0:T(8,128)S(1)}, u32[]{:S(2)}) copy-start(f32[2,16,3,128]{3,1,2,0:T(8,128)S(1)} %get-tuple-element.577) | copy-start | bytes 147460 | tf_op jit(solution)/shard_map/while
  104.4 5.1 %copy-start.8 = (s32[2048]{0:T(1024)S(1)}, s32[2048]{0:T(1024)}, u32[]{:S(2)}) copy-start(s32[2048]{0:T(1024)} %dynamic-slice_bitcast_fusion.5) | copy-start | bytes 24580 | tf_op jit(solution)/shard_map/while
  104.4 5.1 %copy-start.10 = (s32[2,2,256]{2,1,0:T(2,128)S(1)}, s32[2,2,256]{2,1,0:T(2,128)}, u32[]{:S(2)}) copy-start(s32[2,2,256]{2,1,0:T(2,128)} %multiply_add_fusion.23) | copy-start | bytes 12292 | tf_op jit(solution)/shard_map/while
  109.4 8.8 %copy-start.5 = (f32[2,16,3,128]{3,1,2,0:T(8,128)S(1)}, f32[2,16,3,128]{3,1,2,0:T(8,128)}, u32[]{:S(2)}) copy-start(f32[2,16,3,128]{3,1,2,0:T(8,128)} %copy-done.4) | copy-start | bytes 147460 | tf_op jit(solution)/shard_map/while
  109.4 8.8 %copy-start.7 = (f32[2,16,2,128]{3,2,1,0:T(2,128)S(1)}, f32[2,16,2,128]{3,2,1,0:T(2,128)}, u32[]{:S(2)}) copy-start(f32[2,16,2,128]{3,2,1,0:T(2,128)} %copy-done.6) | copy-start | bytes 98308 | tf_op jit(solution)/shard_map/while
  109.5 8.8 %copy-start.15 = (s32[2,16]{1,0:T(2,128)S(1)}, s32[2,16]{1,0:T(2,128)}, u32[]{:S(2)}) copy-start(s32[2,16]{1,0:T(2,128)} %copy-done.14) | copy-start | bytes 388 | tf_op jit(solution)/shard_map/while
  127.1 5.6 %collective-permute-start = (f32[1,2,3,1,5,5,256]{6,3,5,4,2,1,0:T(1,128)S(1)}, f32[1,2,3,1,5,5,256]{6,3,5,4,2,1,0:T(1,128)S(1)}, u32[]{:S(2)}, u32[]{:S(2)}) collective-permute-start(f32[1,2,3,1,5,5,256]{6,3,5,4,2,1,0:T(1,128)S(1)} %get-tuple-element.412), channel_id=1, source_target_pairs={{0,8},{8,16},{16,24},{1,9},{9,17},{17,25},{2,10},{10,18},{18,26},{... | collective-permute-start | bytes 460808 | tf_op jit(solution)/shard_map/ppermute | solution.py:14
  130.5 6.5 %collective-permute-start.1 = (f32[1,2,3,1,5,5,256]{6,3,5,4,2,1,0:T(1,128)S(1)}, f32[1,2,3,1,5,5,256]{6,3,5,4,2,1,0:T(1,128)S(1)}, u32[]{:S(2)}, u32[]{:S(2)}) collective-permute-start(f32[1,2,3,1,5,5,256]{6,3,5,4,2,1,0:T(1,128)S(1)} %get-tuple-element.413), channel_id=1, source_target_pairs={{8,0},{16,8},{24,16},{9,1},{17,9},{25,17},{10,2},{18,10},{26,18},{... | collective-permute-start | bytes 460808 | tf_op jit(solution)/shard_map/ppermute | solution.py:17
  138.0 11.5 %collective-permute-start.2 = (f32[2,1,3,5,1,5,256]{6,3,5,4,2,1,0:T(8,128)S(1)}, f32[2,1,3,5,1,5,256]{6,3,5,4,2,1,0:T(8,128)S(1)}, u32[]{:S(2)}, u32[]{:S(2)}) collective-permute-start(f32[2,1,3,5,1,5,256]{6,3,5,4,2,1,0:T(8,128)S(1)} %get-tuple-element.416), channel_id=1, source_target_pairs={{0,1},{1,2},{2,3},{3,4},{4,5},{5,6},{6,7},{8,9},{9,10},{10,11},{11... | collective-permute-start | bytes 460808 | tf_op jit(solution)/shard_map/ppermute | solution.py:14
  141.1 10.0 %collective-permute-start.3 = (f32[2,1,3,5,1,5,256]{6,3,5,4,2,1,0:T(8,128)S(1)}, f32[2,1,3,5,1,5,256]{6,3,5,4,2,1,0:T(8,128)S(1)}, u32[]{:S(2)}, u32[]{:S(2)}) collective-permute-start(f32[2,1,3,5,1,5,256]{6,3,5,4,2,1,0:T(8,128)S(1)} %get-tuple-element.417), channel_id=1, source_target_pairs={{1,0},{2,1},{3,2},{4,3},{5,4},{6,5},{7,6},{9,8},{10,9},{11,10},{12... | collective-permute-start | bytes 460808 | tf_op jit(solution)/shard_map/ppermute | solution.py:17
  (9 other events, 22.8 us)
where the time goes:
time: 155 us; the launch traced here: 154 us
  matrix products  42.2 us (27%)
  starting transfers between devices  39.5 us (25%)
  other arithmetic  31.6 us (20%)
  local copies, waits for them, and re-layouts  26.9 us (17%)
  waiting for transfers between devices  13.2 us (9%)
    dot_general x2, matrix products, add_block(): jnp.einsum('ks,sxyz->xykz', contrib, onehot, precision=lax.Precision.HIGH...  17.1 us
    mul x2, local copies, waits for them, and re-layouts, sources(): return (direction[:, None, None, None, :] * shape[None]).reshape(375, -1)  10.1 us
    ppermute x2, starting transfers between devices, with_halo(): lax.ppermute(lax.slice_in_dim(block, block.shape[dim] - width, None, axis...  6.47 us
    all_to_all x1, starting transfers between devices, body(): lax.all_to_all(counts, ('gx', 'gy'), split_axis=1, concat_axis=0, tiled=T...  6.32 us
    dot_general x1, matrix products, back(): jnp.einsum('sc,...pqsz->...pqcz', table, field, precision=lax.Precision.H...  5.9 us
    all_to_all x1, starting transfers between devices, body(): lax.all_to_all(residuals, ('gx', 'gy'), split_axis=1, concat_axis=0, tile...  5.89 us
    dot_general x1, matrix products, back(): jnp.einsum('qb,...pqsz->...pbsz', table, field, precision=lax.Precision.H...  5.89 us
    ppermute x2, waiting for transfers between devices, with_halo(): lax.ppermute(lax.slice_in_dim(block, 0, width, axis=dim), axis, backward)  5.88 us
  transfers between devices with their start and end apart: 9, of which 5 were waited for; matrix products, arithmetic and copies ran while one was open for 21% of the time, Pallas kernels for 0%

commit v1 on v0

--- a/solution.py
+++ b/solution.py
@@ -169,7 +169,15 @@
     field = wavefield.reshape(cells_x, cells_y, 3, 5, 5, 5, depth)
     internal = stiffness(field, moduli)
     floats = (
-        lax.all_to_all(residuals, ("gx", "gy"), split_axis=1, concat_axis=0, tiled=True),
+        jnp.concatenate(
+            lax.all_to_all(
+                jnp.stack(jnp.split(residuals, lax.axis_size(("gx", "gy")), axis=1)),
+                ("gx", "gy"),
+                0,
+                0,
+            ),
+            axis=0,
+        ),
         lax.all_to_all(coords, ("gx", "gy"), split_axis=1, concat_axis=0, tiled=True),
         lax.all_to_all(angles, ("gx", "gy"), split_axis=1, concat_axis=0, tiled=True),
     )

time: 155 us -> 173 us (1.12)
  local copies, waits for them, and re-layouts: 26.9 us -> 43.9 us
  waiting for transfers between devices: 13.2 us -> 15.7 us
    unnamed x19 -> x48, local copies, waits for them, and re-layouts: 2.24 us -> 17.7 us
    all_to_all x1, waiting for transfers between devices: 0.37 us -> 5.09 us  [body(): lax.all_to_all(element_ids, ('gx', 'gy'), split_axis=1, concat_axis=0, ti...]
    all_to_all x1, waiting for transfers between devices: 2.52 us -> 0.28 us  [body(): lax.all_to_all(jnp.stack(jnp.split(residuals, lax.axis_size(('gx', 'gy'))...]
  transfers between devices with their start and end apart: 9 -> 9, of which waited for: 5 -> 5; matrix products, arithmetic and copies ran while one was open for 21% -> 28% of each run, Pallas kernels for 0% -> 0%
where the time goes in v1:
time: 173 us; the launch traced here: 172 us
  local copies, waits for them, and re-layouts  43.9 us (25%)
  matrix products  41.8 us (24%)
  starting transfers between devices  39.5 us (23%)
  other arithmetic  30.2 us (17%)
  waiting for transfers between devices  15.7 us (9%)
    unnamed x48, local copies, waits for them, and re-layouts  17.7 us
    dot_general x2, matrix products, add_block(): jnp.einsum('ks,sxyz->xykz', contrib, onehot, precision=lax.Precision.HIGH...  17.1 us
    mul x2, local copies, waits for them, and re-layouts, sources(): return (direction[:, None, None, None, :] * shape[None]).reshape(375, -1)  10.1 us
    ppermute x2, starting transfers between devices, with_halo(): lax.ppermute(lax.slice_in_dim(block, block.shape[dim] - width, None, axis...  6.46 us
    all_to_all x1, starting transfers between devices, body(): lax.all_to_all(counts, ('gx', 'gy'), split_axis=1, concat_axis=0, tiled=T...  6.32 us
    dot_general x1, matrix products, back(): jnp.einsum('sc,...pqsz->...pqcz', table, field, precision=lax.Precision.H...  5.9 us
    dot_general x1, matrix products, back(): jnp.einsum('qb,...pqsz->...pbsz', table, field, precision=lax.Precision.H...  5.89 us
    all_to_all x1, starting transfers between devices, body(): lax.all_to_all(element_ids, ('gx', 'gy'), split_axis=1, concat_axis=0, ti...  5.88 us
  transfers between devices with their start and end apart: 9, of which 5 were waited for; matrix products, arithmetic and copies ran while one was open for 28% of the time, Pallas kernels for 0%

profile of v1, /device:TPU:9, one launch (start us, length us, event | category | flops | bytes accessed | tf_op | source)
XLA Modules:
  0.0 171.8 jit_solution(2392714602216225022)
XLA Ops:
  1.5 6.3 %all-to-all-start.2 = ((s32[1,32,1]{2,0,1:T(1,128)}), s32[1,32,1]{2,0,1:T(1,128)S(1)}, u32[]{:S(2)}, u32[]{:S(2)}) async-start(s32[1,32,1]{2,0,1:T(1,128)} %copy.66), calls=%async_computation.2 | async-start | bytes 32768 | tf_op jit(solution)/shard_map/all_to_all | solution.py:186
  7.8 3.1 %fusion.33 = f32[5,2,2,3,5,5,256]{6,0,5,4,3,2,1:T(8,128)S(1)} fusion(f32[5,5,1,1,1,1,1]{1,0,6,5,4,3,2:T(8,128)} %constant.255, f32[2,2,3,5,5,5,256]{6,1,5,4,3,2,0:T(2,128)S(1)} %bitcast.174), kind=kOutput, calls=%fused_computation.120 | convolution fusion | flops 23040000 | bytes 3072100 | tf_op jit(solution)/shard_map/sc,...pqcz->...pqsz/dot_general | solution.py:97
  37.2 5.9 %all-to-all-start = ((s32[1,32,128]{2,0,1:T(1,128)}), s32[1,32,128]{2,0,1:T(1,128)}, u32[]{:S(2)}, u32[]{:S(2)}) async-start(s32[1,32,128]{2,0,1:T(1,128)} %bitcast), calls=%async_computation | async-start | bytes 32768 | tf_op jit(solution)/shard_map/all_to_all | solution.py:185
  43.6 5.1 %all-to-all-done = s32[1,32,128]{2,0,1:T(1,128)} async-done(((s32[1,32,128]{2,0,1:T(1,128)}), s32[1,32,128]{2,0,1:T(1,128)}, u32[]{:S(2)}, u32[]{:S(2)}) %all-to-all-start) | async-done | bytes 16416 | tf_op jit(solution)/shard_map/all_to_all | solution.py:185
  48.7 4.4 %all-to-all-start.3 = ((f32[32,1,1,128]{3,2,1,0:T(1,128)}), f32[32,1,1,128]{3,2,1,0:T(1,128)}, u32[]{:S(2)}, u32[]{:S(2)}) async-start(f32[32,1,1,128]{3,2,1,0:T(1,128)} %constant_dynamic-update-slice_fusion), calls=%async_computation.3 | async-start | bytes 32768 | tf_op jit(solution)/shard_map/all_to_all | solution.py:173
  53.2 4.6 %pad_maximum_fusion = (f32[2,2,3,5,5,5,256]{6,3,5,4,2,1,0:T(8,128)}, f32[2,2,3,5,5,5,256]{6,3,5,4,2,1,0:T(8,128)}) fusion(f32[2,2,1,5,5,5,256]{6,3,5,4,2,1,0:T(8,128)} %get-tuple-element.403, f32[2,2,1,5,5,5,256]{6,3,5,4,2,1,0:T(8,128)} %get-tuple-element.418, f32[2,2,1,5,5,5,256]{6,3,5,4,2,1,0:T(8,128)S(1)} %get-tuple-element.401, ...), kind=kLoop, calls=%fused_computation.107 | loop fusion | flops 1536000 | bytes 5632000 | tf_op jit(solution)/shard_map/stack | solution.py:126
  58.7 5.6 %all-to-all-start.4 = ((f32[1,32,3,128]{3,2,0,1:T(4,128)}), f32[1,32,3,128]{3,2,0,1:T(4,128)S(1)}, u32[]{:S(2)}, u32[]{:S(2)}) async-start(f32[1,32,3,128]{3,2,0,1:T(4,128)} %copy.67), calls=%async_computation.4 | async-start | bytes 131072 | tf_op jit(solution)/shard_map/all_to_all | solution.py:181
  64.4 5.9 %fusion.31 = f32[2,2,3,5,5,256,5]{5,6,4,3,2,1,0:T(8,128)} fusion(f32[5,5,1,1,1,1,1]{1,0,6,5,4,3,2:T(8,128)S(1)} %copy-done.7, f32[2,2,3,5,5,5,256]{6,3,5,4,2,1,0:T(8,128)} %get-tuple-element.420), kind=kOutput, calls=%fused_computation.117 | convolution fusion | flops 23040000 | bytes 3072100 | tf_op jit(solution)/shard_map/qb,...pqsz->...pbsz/dot_general | solution.py:104
  70.3 5.8 %all-to-all-start.1 = ((f32[1,32,2,128]{3,2,0,1:T(2,128)}), f32[1,32,2,128]{3,2,0,1:T(2,128)S(1)}, u32[]{:S(2)}, u32[]{:S(2)}) async-start(f32[1,32,2,128]{3,2,0,1:T(2,128)} %bitcast.2), calls=%async_computation.1 | async-start | bytes 65536 | tf_op jit(solution)/shard_map/all_to_all | solution.py:182
  76.1 5.9 %fusion.29 = f32[2,2,3,5,5,256,5]{5,6,4,3,2,1,0:T(8,128)} fusion(f32[5,5,1,1,1,1,1]{1,0,6,5,4,3,2:T(8,128)S(1)} %copy-done.7, f32[2,2,3,5,5,5,256]{6,3,5,4,2,1,0:T(8,128)} %get-tuple-element.421), kind=kOutput, calls=%fused_computation.115 | convolution fusion | flops 23040000 | bytes 3072100 | tf_op jit(solution)/shard_map/sc,...pqsz->...pqcz/dot_general | solution.py:105
  82.8 53.7 %while.17 = (s32[]{:T(128)}, f32[2,2,375,256]{3,2,1,0:T(8,128)}, s32[2,16,128]{2,1,0:T(8,128)}, f32[2,16,2,128]{3,2,1,0:T(2,128)S(1)}, s32[2,16]{1,0:T(2,128)S(1...) while((s32[]{:T(128)}, f32[2,2,375,256]{3,2,1,0:T(8,128)}, ...), condition=%wide.region_1.2_spmd.clone, body=%wide.region_0.1_spmd.clone.sunk | while | flops 9442392064 | bytes 20555300 | solution.py:202
  93.0 2.9 %broadcast_multiply_fusion.15 = f32[3,5,5,5,2048]{4,3,2,1,0:T(8,128)} fusion(f32[5,5,5,2048]{3,2,1,0:T(8,128)S(1)} %multiply_add_fusion.22, f32[3,2048]{1,0:T(4,128)S(1)} %maximum_multiply_fusion.2), kind=kLoop, calls=%fused_computation.6.clone.1 | loop fusion | flops 768000 | bytes 4120576 | tf_op jit(solution)/shard_map/while/body/eval_jaxpr/mul | solution.py:89
  95.8 5.1 %reshape.2469 = f32[375,2048,1,1]{1,0,2,3:T(8,128)} reshape(f32[3,5,5,5,2048]{4,3,2,1,0:T(8,128)} %broadcast_multiply_fusion.15) | data formatting | bytes 6144000 | tf_op jit(solution)/shard_map/while/body/eval_jaxpr/mul | solution.py:89
  100.9 8.3 %bitcast_add_fusion.4 = f32[2,2,375,256]{3,2,1,0:T(8,128)} fusion(f32[2,2,375,256]{3,2,1,0:T(8,128)} %get-tuple-element.563, f32[375,2048,1,1]{1,0,2,3:T(8,128)} %reshape.2469, s32[2,2,256]{2,1,0:T(2,128)S(1)} %copy-done.8, s32[2048]{0:T(1024)S(1)} %copy-done.6, pred[]{:T(512)S(6)} %compare.5), kind=kOutput, calls=%fused_computation.8.clone.1 | convolution fusion | flops 9440049152 | bytes 6156289 | tf_op jit(solution)/shard_map/while/body/eval_jaxpr/ks,sxyz->xykz/dot_general | solution.py:199
  119.5 2.9 %broadcast_multiply_fusion.15 = f32[3,5,5,5,2048]{4,3,2,1,0:T(8,128)} fusion(f32[5,5,5,2048]{3,2,1,0:T(8,128)S(1)} %multiply_add_fusion.22, f32[3,2048]{1,0:T(4,128)S(1)} %maximum_multiply_fusion.2), kind=kLoop, calls=%fused_computation.6.clone.1 | loop fusion | flops 768000 | bytes 4120576 | tf_op jit(solution)/shard_map/while/body/eval_jaxpr/mul | solution.py:89
  122.4 5.1 %reshape.2469 = f32[375,2048,1,1]{1,0,2,3:T(8,128)} reshape(f32[3,5,5,5,2048]{4,3,2,1,0:T(8,128)} %broadcast_multiply_fusion.15) | data formatting | bytes 6144000 | tf_op jit(solution)/shard_map/while/body/eval_jaxpr/mul | solution.py:89
  127.5 8.8 %bitcast_add_fusion.4 = f32[2,2,375,256]{3,2,1,0:T(8,128)} fusion(f32[2,2,375,256]{3,2,1,0:T(8,128)} %get-tuple-element.563, f32[375,2048,1,1]{1,0,2,3:T(8,128)} %reshape.2469, s32[2,2,256]{2,1,0:T(2,128)S(1)} %copy-done.8, s32[2048]{0:T(1024)S(1)} %copy-done.6, pred[]{:T(512)S(6)} %compare.5), kind=kOutput, calls=%fused_computation.8.clone.1 | convolution fusion | flops 9440049152 | bytes 6156289 | tf_op jit(solution)/shard_map/while/body/eval_jaxpr/ks,sxyz->xykz/dot_general | solution.py:199
  136.5 2.3 %copy.71 = f32[2,2,375,256]{3,1,2,0:T(2,128)S(1)} copy(f32[2,2,375,256]{3,2,1,0:T(8,128)} %get-tuple-element.295) | data formatting | bytes 3072000 | tf_op jit(solution)/shard_map/while | solution.py:202
  138.9 5.3 %fusion.28 = f32[2,2,3,5,5,5,256]{6,3,5,4,2,1,0:T(8,128)S(1)} fusion(f32[2,2,3,5,5,5,256]{6,1,5,4,3,2,0:T(2,128)S(1)} %bitcast.179, f32[2,2,3,5,5,256,5]{5,6,4,3,2,1,0:T(8,128)} %fusion.29, f32[2,2,3,5,5,256,5]{5,6,4,3,2,1,0:T(8,128)S(1)} %copy-done.1, f32[5,5,1,1,1,1,1]{1,0,6,5,4,3,2:T(8,128)S(1)} %copy-done.7, ...), kind=kOutput, calls=%fused_computation.113 | convolution fusion | flops 24960000 | bytes 7680100 | tf_op jit(solution)/shard_map/pa,...pqsz->...aqsz/dot_general | solution.py:102
  144.6 3.4 %collective-permute-start = (f32[1,2,3,1,5,5,256]{6,3,5,4,2,1,0:T(1,128)S(1)}, f32[1,2,3,1,5,5,256]{6,3,5,4,2,1,0:T(1,128)S(1)}, u32[]{:S(2)}, u32[]{:S(2)}) collective-permute-start(f32[1,2,3,1,5,5,256]{6,3,5,4,2,1,0:T(1,128)S(1)} %get-tuple-element.412), channel_id=1, source_target_pairs={{0,8},{8,16},{16,24},{1,9},{9,17},{17,25},{2,10},{10,18},{18,26},{... | collective-permute-start | bytes 460808 | tf_op jit(solution)/shard_map/ppermute | solution.py:14
  150.3 4.3 %collective-permute-done.1 = f32[1,2,3,1,5,5,256]{6,3,5,4,2,1,0:T(1,128)S(1)} collective-permute-done((f32[1,2,3,1,5,5,256]{6,3,5,4,2,1,0:T(1,128)S(1)}, f32[1,2,3,1,5,5,256]{6,3,5,4,2,1,0:T(1,128)S(1)}, u32[]{:S(2)}, u32[]{:S(2)}) %collective-permute-start.1) | collective-permute-done | bytes 153632 | tf_op jit(solution)/shard_map/ppermute | solution.py:17
  155.5 3.1 %collective-permute-start.2 = (f32[2,1,3,5,1,5,256]{6,3,5,4,2,1,0:T(8,128)S(1)}, f32[2,1,3,5,1,5,256]{6,3,5,4,2,1,0:T(8,128)S(1)}, u32[]{:S(2)}, u32[]{:S(2)}) collective-permute-start(f32[2,1,3,5,1,5,256]{6,3,5,4,2,1,0:T(8,128)S(1)} %get-tuple-element.416), channel_id=1, source_target_pairs={{0,1},{1,2},{2,3},{3,4},{4,5},{5,6},{6,7},{8,9},{9,10},{10,11},{11... | collective-permute-start | bytes 460808 | tf_op jit(solution)/shard_map/ppermute | solution.py:14
  158.6 3.1 %collective-permute-start.3 = (f32[2,1,3,5,1,5,256]{6,3,5,4,2,1,0:T(8,128)S(1)}, f32[2,1,3,5,1,5,256]{6,3,5,4,2,1,0:T(8,128)S(1)}, u32[]{:S(2)}, u32[]{:S(2)}) collective-permute-start(f32[2,1,3,5,1,5,256]{6,3,5,4,2,1,0:T(8,128)S(1)} %get-tuple-element.417), channel_id=1, source_target_pairs={{1,0},{2,1},{3,2},{4,3},{5,4},{6,5},{7,6},{9,8},{10,9},{11,10},{12... | collective-permute-start | bytes 460808 | tf_op jit(solution)/shard_map/ppermute | solution.py:17
  162.6 4.4 %collective-permute-done.2 = f32[2,1,3,5,1,5,256]{6,3,5,4,2,1,0:T(8,128)S(1)} collective-permute-done((f32[2,1,3,5,1,5,256]{6,3,5,4,2,1,0:T(8,128)S(1)}, f32[2,1,3,5,1,5,256]{6,3,5,4,2,1,0:T(8,128)S(1)}, u32[]{:S(2)}, u32[]{:S(2)}) %collective-permute-start.2) | collective-permute-done | bytes 153632 | tf_op jit(solution)/shard_map/ppermute | solution.py:14
  (158 shorter events, 59.6 us)
Async XLA Ops:
  0.0 7.8 %copy-start = (f32[2,2,3,125,256]{4,1,3,2,0:T(2,128)S(1)}, f32[2,2,3,125,256]{4,1,3,2,0:T(2,128)}, u32[]{:S(2)}) copy-start(f32[2,2,3,125,256]{4,1,3,2,0:T(2,128)} %param.11) | copy-start | bytes 4608004
  1.5 35.8 %all-to-all-start.2 = ((s32[1,32,1]{2,0,1:T(1,128)}), s32[1,32,1]{2,0,1:T(1,128)S(1)}, u32[]{:S(2)}, u32[]{:S(2)}) async-start(s32[1,32,1]{2,0,1:T(1,128)} %copy.66), calls=%async_computation.2 | async-start | bytes 32768 | tf_op jit(solution)/shard_map/all_to_all | solution.py:186
  37.2 11.5 %all-to-all-start = ((s32[1,32,128]{2,0,1:T(1,128)}), s32[1,32,128]{2,0,1:T(1,128)}, u32[]{:S(2)}, u32[]{:S(2)}) async-start(s32[1,32,128]{2,0,1:T(1,128)} %bitcast), calls=%async_computation | async-start | bytes 32768 | tf_op jit(solution)/shard_map/all_to_all | solution.py:185
  48.7 10.0 %all-to-all-start.3 = ((f32[32,1,1,128]{3,2,1,0:T(1,128)}), f32[32,1,1,128]{3,2,1,0:T(1,128)}, u32[]{:S(2)}, u32[]{:S(2)}) async-start(f32[32,1,1,128]{3,2,1,0:T(1,128)} %constant_dynamic-update-slice_fusion), calls=%async_computation.3 | async-start | bytes 32768 | tf_op jit(solution)/shard_map/all_to_all | solution.py:173
  58.7 11.6 %all-to-all-start.4 = ((f32[1,32,3,128]{3,2,0,1:T(4,128)}), f32[1,32,3,128]{3,2,0,1:T(4,128)S(1)}, u32[]{:S(2)}, u32[]{:S(2)}) async-start(f32[1,32,3,128]{3,2,0,1:T(4,128)} %copy.67), calls=%async_computation.4 | async-start | bytes 131072 | tf_op jit(solution)/shard_map/all_to_all | solution.py:181
  70.3 12.4 %all-to-all-start.1 = ((f32[1,32,2,128]{3,2,0,1:T(2,128)}), f32[1,32,2,128]{3,2,0,1:T(2,128)S(1)}, u32[]{:S(2)}, u32[]{:S(2)}) async-start(f32[1,32,2,128]{3,2,0,1:T(2,128)} %bitcast.2), calls=%async_computation.1 | async-start | bytes 65536 | tf_op jit(solution)/shard_map/all_to_all | solution.py:182
  82.8 4.8 %copy-start.2 = (f32[2,16,3,128]{3,1,2,0:T(8,128)}, f32[2,16,3,128]{3,1,2,0:T(8,128)S(1)}, u32[]{:S(2)}) copy-start(f32[2,16,3,128]{3,1,2,0:T(8,128)S(1)} %get-tuple-element.577) | copy-start | bytes 147460 | tf_op jit(solution)/shard_map/while
  82.8 4.8 %copy-start.4 = (f32[2,16,2,128]{3,2,1,0:T(2,128)}, f32[2,16,2,128]{3,2,1,0:T(2,128)S(1)}, u32[]{:S(2)}) copy-start(f32[2,16,2,128]{3,2,1,0:T(2,128)S(1)} %get-tuple-element.574) | copy-start | bytes 98308 | tf_op jit(solution)/shard_map/while
  95.8 5.1 %copy-start.6 = (s32[2048]{0:T(1024)S(1)}, s32[2048]{0:T(1024)}, u32[]{:S(2)}) copy-start(s32[2048]{0:T(1024)} %dynamic-slice_bitcast_fusion.5) | copy-start | bytes 24580 | tf_op jit(solution)/shard_map/while
  95.8 5.1 %copy-start.8 = (s32[2,2,256]{2,1,0:T(2,128)S(1)}, s32[2,2,256]{2,1,0:T(2,128)}, u32[]{:S(2)}) copy-start(s32[2,2,256]{2,1,0:T(2,128)} %multiply_add_fusion.23) | copy-start | bytes 12292 | tf_op jit(solution)/shard_map/while
  100.9 8.4 %copy-start.3 = (f32[2,16,3,128]{3,1,2,0:T(8,128)S(1)}, f32[2,16,3,128]{3,1,2,0:T(8,128)}, u32[]{:S(2)}) copy-start(f32[2,16,3,128]{3,1,2,0:T(8,128)} %copy-done.2) | copy-start | bytes 147460 | tf_op jit(solution)/shard_map/while
  100.9 8.4 %copy-start.5 = (f32[2,16,2,128]{3,2,1,0:T(2,128)S(1)}, f32[2,16,2,128]{3,2,1,0:T(2,128)}, u32[]{:S(2)}) copy-start(f32[2,16,2,128]{3,2,1,0:T(2,128)} %copy-done.4) | copy-start | bytes 98308 | tf_op jit(solution)/shard_map/while
  100.9 8.4 %copy-start.14 = (s32[2,16]{1,0:T(2,128)S(1)}, s32[2,16]{1,0:T(2,128)}, u32[]{:S(2)}) copy-start(s32[2,16]{1,0:T(2,128)} %copy-done.13) | copy-start | bytes 388 | tf_op jit(solution)/shard_map/while
  109.3 4.8 %copy-start.2 = (f32[2,16,3,128]{3,1,2,0:T(8,128)}, f32[2,16,3,128]{3,1,2,0:T(8,128)S(1)}, u32[]{:S(2)}) copy-start(f32[2,16,3,128]{3,1,2,0:T(8,128)S(1)} %get-tuple-element.577) | copy-start | bytes 147460 | tf_op jit(solution)/shard_map/while
  109.3 4.8 %copy-start.4 = (f32[2,16,2,128]{3,2,1,0:T(2,128)}, f32[2,16,2,128]{3,2,1,0:T(2,128)S(1)}, u32[]{:S(2)}) copy-start(f32[2,16,2,128]{3,2,1,0:T(2,128)S(1)} %get-tuple-element.574) | copy-start | bytes 98308 | tf_op jit(solution)/shard_map/while
  122.4 5.1 %copy-start.6 = (s32[2048]{0:T(1024)S(1)}, s32[2048]{0:T(1024)}, u32[]{:S(2)}) copy-start(s32[2048]{0:T(1024)} %dynamic-slice_bitcast_fusion.5) | copy-start | bytes 24580 | tf_op jit(solution)/shard_map/while
  122.4 5.1 %copy-start.8 = (s32[2,2,256]{2,1,0:T(2,128)S(1)}, s32[2,2,256]{2,1,0:T(2,128)}, u32[]{:S(2)}) copy-start(s32[2,2,256]{2,1,0:T(2,128)} %multiply_add_fusion.23) | copy-start | bytes 12292 | tf_op jit(solution)/shard_map/while
  127.4 8.8 %copy-start.3 = (f32[2,16,3,128]{3,1,2,0:T(8,128)S(1)}, f32[2,16,3,128]{3,1,2,0:T(8,128)}, u32[]{:S(2)}) copy-start(f32[2,16,3,128]{3,1,2,0:T(8,128)} %copy-done.2) | copy-start | bytes 147460 | tf_op jit(solution)/shard_map/while
  127.4 8.8 %copy-start.5 = (f32[2,16,2,128]{3,2,1,0:T(2,128)S(1)}, f32[2,16,2,128]{3,2,1,0:T(2,128)}, u32[]{:S(2)}) copy-start(f32[2,16,2,128]{3,2,1,0:T(2,128)} %copy-done.4) | copy-start | bytes 98308 | tf_op jit(solution)/shard_map/while
  127.5 8.8 %copy-start.14 = (s32[2,16]{1,0:T(2,128)S(1)}, s32[2,16]{1,0:T(2,128)}, u32[]{:S(2)}) copy-start(s32[2,16]{1,0:T(2,128)} %copy-done.13) | copy-start | bytes 388 | tf_op jit(solution)/shard_map/while
  144.6 5.6 %collective-permute-start = (f32[1,2,3,1,5,5,256]{6,3,5,4,2,1,0:T(1,128)S(1)}, f32[1,2,3,1,5,5,256]{6,3,5,4,2,1,0:T(1,128)S(1)}, u32[]{:S(2)}, u32[]{:S(2)}) collective-permute-start(f32[1,2,3,1,5,5,256]{6,3,5,4,2,1,0:T(1,128)S(1)} %get-tuple-element.412), channel_id=1, source_target_pairs={{0,8},{8,16},{16,24},{1,9},{9,17},{17,25},{2,10},{10,18},{18,26},{... | collective-permute-start | bytes 460808 | tf_op jit(solution)/shard_map/ppermute | solution.py:14
  148.0 6.5 %collective-permute-start.1 = (f32[1,2,3,1,5,5,256]{6,3,5,4,2,1,0:T(1,128)S(1)}, f32[1,2,3,1,5,5,256]{6,3,5,4,2,1,0:T(1,128)S(1)}, u32[]{:S(2)}, u32[]{:S(2)}) collective-permute-start(f32[1,2,3,1,5,5,256]{6,3,5,4,2,1,0:T(1,128)S(1)} %get-tuple-element.413), channel_id=1, source_target_pairs={{8,0},{16,8},{24,16},{9,1},{17,9},{25,17},{10,2},{18,10},{26,18},{... | collective-permute-start | bytes 460808 | tf_op jit(solution)/shard_map/ppermute | solution.py:17
  155.5 11.5 %collective-permute-start.2 = (f32[2,1,3,5,1,5,256]{6,3,5,4,2,1,0:T(8,128)S(1)}, f32[2,1,3,5,1,5,256]{6,3,5,4,2,1,0:T(8,128)S(1)}, u32[]{:S(2)}, u32[]{:S(2)}) collective-permute-start(f32[2,1,3,5,1,5,256]{6,3,5,4,2,1,0:T(8,128)S(1)} %get-tuple-element.416), channel_id=1, source_target_pairs={{0,1},{1,2},{2,3},{3,4},{4,5},{5,6},{6,7},{8,9},{9,10},{10,11},{11... | collective-permute-start | bytes 460808 | tf_op jit(solution)/shard_map/ppermute | solution.py:14
  158.6 10.0 %collective-permute-start.3 = (f32[2,1,3,5,1,5,256]{6,3,5,4,2,1,0:T(8,128)S(1)}, f32[2,1,3,5,1,5,256]{6,3,5,4,2,1,0:T(8,128)S(1)}, u32[]{:S(2)}, u32[]{:S(2)}) collective-permute-start(f32[2,1,3,5,1,5,256]{6,3,5,4,2,1,0:T(8,128)S(1)} %get-tuple-element.417), channel_id=1, source_target_pairs={{1,0},{2,1},{3,2},{4,3},{5,4},{6,5},{7,6},{9,8},{10,9},{11,10},{12... | collective-permute-start | bytes 460808 | tf_op jit(solution)/shard_map/ppermute | solution.py:17
  (8 other events, 18.2 us)
